TPU v7x, 256 devices: a whole 4x4x8 slice. The times are simulated.
256 devices in a mesh: section: 16 (over x, y), expert: 16 (over z, core).
Axes of the slice: x: 4, y: 4, z: 8, core: 2. Of those that a mesh axis runs over, the one named last changes fastest.
Arguments:
- tokens: bfloat16 [8, 128, 2048], P(None, 'expert'), may hold values from -6 to 6
- norm_gain: float32 [8, 2048], replicated, may hold values from 0.1 to 1.9
- w_gate: bfloat16 [16, 2048, 14336], P('section', None, 'expert'), may hold values from -0.125 to 0.125
- w_up: bfloat16 [16, 2048, 14336], P('section', None, 'expert'), may hold values from -0.125 to 0.125
- w_down: bfloat16 [16, 14336, 2048], P('section', 'expert'), may hold values from -0.0625 to 0.0625
- expert_ids: int32 [8, 8, 128, 2], P(None, None, 'expert'), may hold values from 0 to 3, as said below
- slot_ids: int32 [8, 8, 128, 2], P(None, None, 'expert'), may hold values from 0 to 4, as said below
- dropped: int32 [8, 8, 128, 2], P(None, None, 'expert'), may hold values from 0 to 1, as said below
- gate_weights: float32 [8, 8, 128, 2], P(None, None, 'expert'), may hold values from 0.1 to 1
Outputs:
- states: bfloat16 [16, 8, 128, 2048], P('section', None, 'expert')
Inputs may be any that keep to these rules, and one draw needn't show every extreme that they name: `expert_ids`: the two experts of a token differ. `slot_ids`: among the kept choices of the tokens of one index of expert that name one expert, the slots are 0, 1, ... up to their count less one, each once. At most 5 kept choices of the tokens of one index of expert name one expert, and a choice is dropped only where 5 kept choices of its index of expert name its expert; in each layer and micro-batch some expert receives exactly 5 kept choices from every index of expert.
All inputs are finite; a program needn't handle non-finite values.
Results may differ from a plain program's by a relative error of at most 0.025.
Values may be sent and summed in bfloat16 or wider, within the bound.
A program may use at most 64 MiB of HBM per device.

v0:
```python
import jax
import jax.numpy as jnp
from jax import lax
from jax.sharding import PartitionSpec as P

EXPERTS = 4


def shortened(value):
    return jax.tree.map(lambda a: a.astype(jnp.bfloat16) if a.dtype == jnp.float32 else a, value)


def shifted(value, axis, by):
    size = lax.axis_size(axis)
    pairs = [(i, i + by) for i in range(size) if 0 <= i + by < size]
    return lax.ppermute(value, axis, pairs)


def on_device(tokens, norm_gain, w_gate, w_up, w_down, expert_ids, slot_ids, dropped, gate_weights):
    groups = lax.axis_size("expert")
    sections = lax.axis_size("section")
    section_at = lax.axis_index("section")
    local_count = EXPERTS // 2
    shards = groups // local_count
    micro_count, tok_rows, model_width = tokens.shape
    capacity = 5 * tok_rows // (2 * EXPERTS)
    slot_limit = local_count * capacity
    layer_at = section_at // 2
    half_at = section_at % 2
    odd_section = half_at == 1
    gain_row = lax.dynamic_index_in_dim(norm_gain, layer_at, 0, keepdims=False)
    gate_mat = w_gate[0]
    up_mat = w_up[0]
    down_mat = w_down[0]
    route_all = lax.dynamic_index_in_dim(expert_ids, layer_at, 0, keepdims=False)
    slot_all = lax.dynamic_index_in_dim(slot_ids, layer_at, 0, keepdims=False)
    drop_all = lax.dynamic_index_in_dim(dropped, layer_at, 0, keepdims=False)
    weigh_all = lax.dynamic_index_in_dim(gate_weights, layer_at, 0, keepdims=False)

    def expert_rows(received):
        flat_rows = received.reshape(-1, model_width)
        gate_vals = jnp.dot(flat_rows, gate_mat, preferred_element_type=jnp.float32)
        up_vals = jnp.dot(flat_rows, up_mat, preferred_element_type=jnp.float32)
        hidden = (jax.nn.silu(gate_vals) * up_vals).astype(jnp.bfloat16)
        partial_rows = jnp.dot(hidden, down_mat, preferred_element_type=jnp.float32).astype(
            jnp.bfloat16
        )
        return partial_rows.reshape(received.shape)

    def skip_rows(received):
        return jnp.zeros(received.shape, jnp.bfloat16)

    def run_experts(outgoing, active):
        received = lax.all_to_all(outgoing, "expert", split_axis=0, concat_axis=0, tiled=True)
        computed = lax.cond(active, expert_rows, skip_rows, received)
        returned = lax.all_to_all(computed, "expert", split_axis=0, concat_axis=0, tiled=True)
        return returned

    def advance(tick_count, carry):
        incoming, states = carry
        micro_at = tick_count - section_at
        active = (micro_at >= 0) & (micro_at < micro_count)
        micro_index = jnp.clip(micro_at, 0, micro_count - 1)
        fresh_rows = lax.dynamic_index_in_dim(tokens, micro_index, 0, keepdims=False)
        route_now = lax.dynamic_index_in_dim(route_all, micro_index, 0, keepdims=False)
        slot_now = lax.dynamic_index_in_dim(slot_all, micro_index, 0, keepdims=False)
        drop_now = lax.dynamic_index_in_dim(drop_all, micro_index, 0, keepdims=False)
        weigh_now = lax.dynamic_index_in_dim(weigh_all, micro_index, 0, keepdims=False)
        kept_mask = drop_now == 0
        passed_state = incoming[0]
        prior_rows = [incoming[1], incoming[2]]
        current = jnp.where(section_at == 0, fresh_rows, passed_state)
        wide_rows = current.astype(jnp.float32)
        inv_scale = lax.rsqrt(jnp.mean(wide_rows * wide_rows, axis=-1, keepdims=True) + 1e-05)
        normed = (wide_rows * inv_scale * gain_row).astype(jnp.bfloat16)
        local_id = route_now - half_at * local_count
        owned = kept_mask & (local_id >= 0) & (local_id < local_count)
        target = jnp.where(owned, local_id * capacity + slot_now, slot_limit)
        buffer = jnp.zeros((slot_limit, model_width), jnp.bfloat16)
        buffer = buffer.at[target[:, 0]].set(normed, mode="drop")
        buffer = buffer.at[target[:, 1]].set(normed, mode="drop")
        buffer = buffer.reshape(local_count, capacity, model_width)
        outgoing = jnp.repeat(buffer, shards, axis=0)
        returned = run_experts(outgoing, active)
        summed = jnp.sum(
            returned.astype(jnp.float32).reshape(local_count, shards, capacity, model_width), axis=1
        )
        flat_back = summed.astype(jnp.bfloat16).reshape(slot_limit, model_width)
        clipped = jnp.minimum(target, slot_limit - 1)
        combined = wide_rows
        chosen_rows = []
        for member in range(2):
            own_rows = flat_back[clipped[:, member]]
            chosen = jnp.where(owned[:, member : member + 1], own_rows, prior_rows[member])
            chosen_rows.append(chosen)
            combined = combined + weigh_now[:, member : member + 1] * chosen.astype(jnp.float32)
        mixed_rows = combined.astype(jnp.bfloat16)
        updated = lax.dynamic_update_index_in_dim(states, mixed_rows, micro_index, 0)
        states = jnp.where(active, updated, states)
        zero_rows = jnp.zeros_like(current)
        even_load = jnp.stack([current, chosen_rows[0], chosen_rows[1]])
        odd_load = jnp.stack([mixed_rows, zero_rows, zero_rows])
        payload = jnp.where(odd_section, odd_load, even_load)
        passed = shifted(shortened(payload), "section", 1).astype(payload.dtype)
        return (passed, states)

    start_load = jnp.zeros((3, tok_rows, model_width), jnp.bfloat16)
    initial = (start_load, jnp.zeros((micro_count, tok_rows, model_width), jnp.bfloat16))
    final_load, states = lax.fori_loop(0, micro_count + sections - 1, advance, initial)
    return states[None]


def solution(mesh):
    return jax.shard_map(
        on_device,
        mesh=mesh,
        in_specs=(
            P(None, "expert", None),
            P(),
            P("section", None, "expert"),
            P("section", None, "expert"),
            P("section", "expert", None),
            P(None, None, "expert", None),
            P(None, None, "expert", None),
            P(None, None, "expert", None),
            P(None, None, "expert", None),
        ),
        out_specs=P("section", None, "expert", None),
        check_vma=False,
    )
```

profile of v0, /device:TPU:30, one launch (start us, length us, event | category | flops | bytes accessed | tf_op | source)
XLA Modules:
  0.0 1398.6 jit_solution(9079945764367252696)
XLA Ops:
  2.2 1395.6 %while.17 = (s32[]{:T(128)}, bf16[3,8,2048]{2,1,0:T(8,128)(2,1)S(1)}, bf16[8,8,2048]{2,1,0:T(8,128)(2,1)S(1)}, pred[]{:T(512)}, pred[]{:T(512)}, /*index=5*/s32[...) while((s32[]{:T(128)}, ...), condition=%wide.region_7.8_spmd, body=%wide.region_0.7_spmd.sunk | while | flops 882067776 | bytes 18887540 | solution.py:109
  14.3 15.9 %all-to-all-done = bf16[16,5,2048]{2,1,0:T(8,128)(2,1)S(1)} async-done(((bf16[16,5,2048]{2,1,0:T(8,128)(2,1)}), bf16[16,5,2048]{2,1,0:T(8,128)(2,1)S(1)}, u32[]{:S(2)}, u32[]{:S(2)}) %all-to-all-start) | async-done | bytes 327712 | tf_op jit(solution)/shard_map/while/body/eval_jaxpr/all_to_all | solution.py:54
  35.3 16.1 %all-to-all-done.1 = bf16[16,5,2048]{2,1,0:T(8,128)(2,1)S(1)} async-done(((bf16[16,5,2048]{2,1,0:T(8,128)(2,1)}), bf16[16,5,2048]{2,1,0:T(8,128)(2,1)S(1)}, u32[]{:S(2)}, u32[]{:S(2)}) %all-to-all-start.1) | async-done | bytes 327712 | tf_op jit(solution)/shard_map/while/body/eval_jaxpr/all_to_all | solution.py:56
  67.1 15.9 %all-to-all-done = bf16[16,5,2048]{2,1,0:T(8,128)(2,1)S(1)} async-done(((bf16[16,5,2048]{2,1,0:T(8,128)(2,1)}), bf16[16,5,2048]{2,1,0:T(8,128)(2,1)S(1)}, u32[]{:S(2)}, u32[]{:S(2)}) %all-to-all-start) | async-done | bytes 327712 | tf_op jit(solution)/shard_map/while/body/eval_jaxpr/all_to_all | solution.py:54
  88.1 16.1 %all-to-all-done.1 = bf16[16,5,2048]{2,1,0:T(8,128)(2,1)S(1)} async-done(((bf16[16,5,2048]{2,1,0:T(8,128)(2,1)}), bf16[16,5,2048]{2,1,0:T(8,128)(2,1)S(1)}, u32[]{:S(2)}, u32[]{:S(2)}) %all-to-all-start.1) | async-done | bytes 327712 | tf_op jit(solution)/shard_map/while/body/eval_jaxpr/all_to_all | solution.py:56
  119.8 15.9 %all-to-all-done = bf16[16,5,2048]{2,1,0:T(8,128)(2,1)S(1)} async-done(((bf16[16,5,2048]{2,1,0:T(8,128)(2,1)}), bf16[16,5,2048]{2,1,0:T(8,128)(2,1)S(1)}, u32[]{:S(2)}, u32[]{:S(2)}) %all-to-all-start) | async-done | bytes 327712 | tf_op jit(solution)/shard_map/while/body/eval_jaxpr/all_to_all | solution.py:54
  140.9 16.1 %all-to-all-done.1 = bf16[16,5,2048]{2,1,0:T(8,128)(2,1)S(1)} async-done(((bf16[16,5,2048]{2,1,0:T(8,128)(2,1)}), bf16[16,5,2048]{2,1,0:T(8,128)(2,1)S(1)}, u32[]{:S(2)}, u32[]{:S(2)}) %all-to-all-start.1) | async-done | bytes 327712 | tf_op jit(solution)/shard_map/while/body/eval_jaxpr/all_to_all | solution.py:56
  172.6 15.9 %all-to-all-done = bf16[16,5,2048]{2,1,0:T(8,128)(2,1)S(1)} async-done(((bf16[16,5,2048]{2,1,0:T(8,128)(2,1)}), bf16[16,5,2048]{2,1,0:T(8,128)(2,1)S(1)}, u32[]{:S(2)}, u32[]{:S(2)}) %all-to-all-start) | async-done | bytes 327712 | tf_op jit(solution)/shard_map/while/body/eval_jaxpr/all_to_all | solution.py:54
  193.7 16.1 %all-to-all-done.1 = bf16[16,5,2048]{2,1,0:T(8,128)(2,1)S(1)} async-done(((bf16[16,5,2048]{2,1,0:T(8,128)(2,1)}), bf16[16,5,2048]{2,1,0:T(8,128)(2,1)S(1)}, u32[]{:S(2)}, u32[]{:S(2)}) %all-to-all-start.1) | async-done | bytes 327712 | tf_op jit(solution)/shard_map/while/body/eval_jaxpr/all_to_all | solution.py:56
  225.4 15.9 %all-to-all-done = bf16[16,5,2048]{2,1,0:T(8,128)(2,1)S(1)} async-done(((bf16[16,5,2048]{2,1,0:T(8,128)(2,1)}), bf16[16,5,2048]{2,1,0:T(8,128)(2,1)S(1)}, u32[]{:S(2)}, u32[]{:S(2)}) %all-to-all-start) | async-done | bytes 327712 | tf_op jit(solution)/shard_map/while/body/eval_jaxpr/all_to_all | solution.py:54
  246.4 16.1 %all-to-all-done.1 = bf16[16,5,2048]{2,1,0:T(8,128)(2,1)S(1)} async-done(((bf16[16,5,2048]{2,1,0:T(8,128)(2,1)}), bf16[16,5,2048]{2,1,0:T(8,128)(2,1)S(1)}, u32[]{:S(2)}, u32[]{:S(2)}) %all-to-all-start.1) | async-done | bytes 327712 | tf_op jit(solution)/shard_map/while/body/eval_jaxpr/all_to_all | solution.py:56
  278.8 15.9 %all-to-all-done = bf16[16,5,2048]{2,1,0:T(8,128)(2,1)S(1)} async-done(((bf16[16,5,2048]{2,1,0:T(8,128)(2,1)}), bf16[16,5,2048]{2,1,0:T(8,128)(2,1)S(1)}, u32[]{:S(2)}, u32[]{:S(2)}) %all-to-all-start) | async-done | bytes 327712 | tf_op jit(solution)/shard_map/while/body/eval_jaxpr/all_to_all | solution.py:54
  299.8 16.1 %all-to-all-done.1 = bf16[16,5,2048]{2,1,0:T(8,128)(2,1)S(1)} async-done(((bf16[16,5,2048]{2,1,0:T(8,128)(2,1)}), bf16[16,5,2048]{2,1,0:T(8,128)(2,1)S(1)}, u32[]{:S(2)}, u32[]{:S(2)}) %all-to-all-start.1) | async-done | bytes 327712 | tf_op jit(solution)/shard_map/while/body/eval_jaxpr/all_to_all | solution.py:56
  333.7 15.9 %all-to-all-done = bf16[16,5,2048]{2,1,0:T(8,128)(2,1)S(1)} async-done(((bf16[16,5,2048]{2,1,0:T(8,128)(2,1)}), bf16[16,5,2048]{2,1,0:T(8,128)(2,1)S(1)}, u32[]{:S(2)}, u32[]{:S(2)}) %all-to-all-start) | async-done | bytes 327712 | tf_op jit(solution)/shard_map/while/body/eval_jaxpr/all_to_all | solution.py:54
  354.7 16.1 %all-to-all-done.1 = bf16[16,5,2048]{2,1,0:T(8,128)(2,1)S(1)} async-done(((bf16[16,5,2048]{2,1,0:T(8,128)(2,1)}), bf16[16,5,2048]{2,1,0:T(8,128)(2,1)S(1)}, u32[]{:S(2)}, u32[]{:S(2)}) %all-to-all-start.1) | async-done | bytes 327712 | tf_op jit(solution)/shard_map/while/body/eval_jaxpr/all_to_all | solution.py:56
  388.5 15.9 %all-to-all-done = bf16[16,5,2048]{2,1,0:T(8,128)(2,1)S(1)} async-done(((bf16[16,5,2048]{2,1,0:T(8,128)(2,1)}), bf16[16,5,2048]{2,1,0:T(8,128)(2,1)S(1)}, u32[]{:S(2)}, u32[]{:S(2)}) %all-to-all-start) | async-done | bytes 327712 | tf_op jit(solution)/shard_map/while/body/eval_jaxpr/all_to_all | solution.py:54
  409.6 16.1 %all-to-all-done.1 = bf16[16,5,2048]{2,1,0:T(8,128)(2,1)S(1)} async-done(((bf16[16,5,2048]{2,1,0:T(8,128)(2,1)}), bf16[16,5,2048]{2,1,0:T(8,128)(2,1)S(1)}, u32[]{:S(2)}, u32[]{:S(2)}) %all-to-all-start.1) | async-done | bytes 327712 | tf_op jit(solution)/shard_map/while/body/eval_jaxpr/all_to_all | solution.py:56
  443.4 15.9 %all-to-all-done = bf16[16,5,2048]{2,1,0:T(8,128)(2,1)S(1)} async-done(((bf16[16,5,2048]{2,1,0:T(8,128)(2,1)}), bf16[16,5,2048]{2,1,0:T(8,128)(2,1)S(1)}, u32[]{:S(2)}, u32[]{:S(2)}) %all-to-all-start) | async-done | bytes 327712 | tf_op jit(solution)/shard_map/while/body/eval_jaxpr/all_to_all | solution.py:54
  464.5 16.1 %all-to-all-done.1 = bf16[16,5,2048]{2,1,0:T(8,128)(2,1)S(1)} async-done(((bf16[16,5,2048]{2,1,0:T(8,128)(2,1)}), bf16[16,5,2048]{2,1,0:T(8,128)(2,1)S(1)}, u32[]{:S(2)}, u32[]{:S(2)}) %all-to-all-start.1) | async-done | bytes 327712 | tf_op jit(solution)/shard_map/while/body/eval_jaxpr/all_to_all | solution.py:56
  498.3 15.9 %all-to-all-done = bf16[16,5,2048]{2,1,0:T(8,128)(2,1)S(1)} async-done(((bf16[16,5,2048]{2,1,0:T(8,128)(2,1)}), bf16[16,5,2048]{2,1,0:T(8,128)(2,1)S(1)}, u32[]{:S(2)}, u32[]{:S(2)}) %all-to-all-start) | async-done | bytes 327712 | tf_op jit(solution)/shard_map/while/body/eval_jaxpr/all_to_all | solution.py:54
  519.4 16.1 %all-to-all-done.1 = bf16[16,5,2048]{2,1,0:T(8,128)(2,1)S(1)} async-done(((bf16[16,5,2048]{2,1,0:T(8,128)(2,1)}), bf16[16,5,2048]{2,1,0:T(8,128)(2,1)S(1)}, u32[]{:S(2)}, u32[]{:S(2)}) %all-to-all-start.1) | async-done | bytes 327712 | tf_op jit(solution)/shard_map/while/body/eval_jaxpr/all_to_all | solution.py:56
  553.2 15.9 %all-to-all-done = bf16[16,5,2048]{2,1,0:T(8,128)(2,1)S(1)} async-done(((bf16[16,5,2048]{2,1,0:T(8,128)(2,1)}), bf16[16,5,2048]{2,1,0:T(8,128)(2,1)S(1)}, u32[]{:S(2)}, u32[]{:S(2)}) %all-to-all-start) | async-done | bytes 327712 | tf_op jit(solution)/shard_map/while/body/eval_jaxpr/all_to_all | solution.py:54
  574.2 16.1 %all-to-all-done.1 = bf16[16,5,2048]{2,1,0:T(8,128)(2,1)S(1)} async-done(((bf16[16,5,2048]{2,1,0:T(8,128)(2,1)}), bf16[16,5,2048]{2,1,0:T(8,128)(2,1)S(1)}, u32[]{:S(2)}, u32[]{:S(2)}) %all-to-all-start.1) | async-done | bytes 327712 | tf_op jit(solution)/shard_map/while/body/eval_jaxpr/all_to_all | solution.py:56
  608.0 15.9 %all-to-all-done = bf16[16,5,2048]{2,1,0:T(8,128)(2,1)S(1)} async-done(((bf16[16,5,2048]{2,1,0:T(8,128)(2,1)}), bf16[16,5,2048]{2,1,0:T(8,128)(2,1)S(1)}, u32[]{:S(2)}, u32[]{:S(2)}) %all-to-all-start) | async-done | bytes 327712 | tf_op jit(solution)/shard_map/while/body/eval_jaxpr/all_to_all | solution.py:54
  629.1 16.1 %all-to-all-done.1 = bf16[16,5,2048]{2,1,0:T(8,128)(2,1)S(1)} async-done(((bf16[16,5,2048]{2,1,0:T(8,128)(2,1)}), bf16[16,5,2048]{2,1,0:T(8,128)(2,1)S(1)}, u32[]{:S(2)}, u32[]{:S(2)}) %all-to-all-start.1) | async-done | bytes 327712 | tf_op jit(solution)/shard_map/while/body/eval_jaxpr/all_to_all | solution.py:56
  662.9 15.9 %all-to-all-done = bf16[16,5,2048]{2,1,0:T(8,128)(2,1)S(1)} async-done(((bf16[16,5,2048]{2,1,0:T(8,128)(2,1)}), bf16[16,5,2048]{2,1,0:T(8,128)(2,1)S(1)}, u32[]{:S(2)}, u32[]{:S(2)}) %all-to-all-start) | async-done | bytes 327712 | tf_op jit(solution)/shard_map/while/body/eval_jaxpr/all_to_all | solution.py:54
  684.0 16.1 %all-to-all-done.1 = bf16[16,5,2048]{2,1,0:T(8,128)(2,1)S(1)} async-done(((bf16[16,5,2048]{2,1,0:T(8,128)(2,1)}), bf16[16,5,2048]{2,1,0:T(8,128)(2,1)S(1)}, u32[]{:S(2)}, u32[]{:S(2)}) %all-to-all-start.1) | async-done | bytes 327712 | tf_op jit(solution)/shard_map/while/body/eval_jaxpr/all_to_all | solution.py:56
  717.8 15.9 %all-to-all-done = bf16[16,5,2048]{2,1,0:T(8,128)(2,1)S(1)} async-done(((bf16[16,5,2048]{2,1,0:T(8,128)(2,1)}), bf16[16,5,2048]{2,1,0:T(8,128)(2,1)S(1)}, u32[]{:S(2)}, u32[]{:S(2)}) %all-to-all-start) | async-done | bytes 327712 | tf_op jit(solution)/shard_map/while/body/eval_jaxpr/all_to_all | solution.py:54
  738.9 16.1 %all-to-all-done.1 = bf16[16,5,2048]{2,1,0:T(8,128)(2,1)S(1)} async-done(((bf16[16,5,2048]{2,1,0:T(8,128)(2,1)}), bf16[16,5,2048]{2,1,0:T(8,128)(2,1)S(1)}, u32[]{:S(2)}, u32[]{:S(2)}) %all-to-all-start.1) | async-done | bytes 327712 | tf_op jit(solution)/shard_map/while/body/eval_jaxpr/all_to_all | solution.py:56
  772.7 15.9 %all-to-all-done = bf16[16,5,2048]{2,1,0:T(8,128)(2,1)S(1)} async-done(((bf16[16,5,2048]{2,1,0:T(8,128)(2,1)}), bf16[16,5,2048]{2,1,0:T(8,128)(2,1)S(1)}, u32[]{:S(2)}, u32[]{:S(2)}) %all-to-all-start) | async-done | bytes 327712 | tf_op jit(solution)/shard_map/while/body/eval_jaxpr/all_to_all | solution.py:54
  793.7 16.1 %all-to-all-done.1 = bf16[16,5,2048]{2,1,0:T(8,128)(2,1)S(1)} async-done(((bf16[16,5,2048]{2,1,0:T(8,128)(2,1)}), bf16[16,5,2048]{2,1,0:T(8,128)(2,1)S(1)}, u32[]{:S(2)}, u32[]{:S(2)}) %all-to-all-start.1) | async-done | bytes 327712 | tf_op jit(solution)/shard_map/while/body/eval_jaxpr/all_to_all | solution.py:56
  812.6 87.6 %collective-permute-done = bf16[3,8,2048]{2,1,0:T(8,128)(2,1)S(1)} collective-permute-done((bf16[3,8,2048]{2,1,0:T(8,128)(2,1)S(1)}, bf16[3,8,2048]{2,1,0:T(8,128)(2,1)S(1)}, u32[]{:S(2)}, u32[]{:S(2)}) %collective-permute-start) | collective-permute-done | bytes 98336 | tf_op jit(solution)/shard_map/while/body/eval_jaxpr/ppermute | solution.py:16
  907.9 15.9 %all-to-all-done = bf16[16,5,2048]{2,1,0:T(8,128)(2,1)S(1)} async-done(((bf16[16,5,2048]{2,1,0:T(8,128)(2,1)}), bf16[16,5,2048]{2,1,0:T(8,128)(2,1)S(1)}, u32[]{:S(2)}, u32[]{:S(2)}) %all-to-all-start) | async-done | bytes 327712 | tf_op jit(solution)/shard_map/while/body/eval_jaxpr/all_to_all | solution.py:54
  936.4 16.1 %all-to-all-done.1 = bf16[16,5,2048]{2,1,0:T(8,128)(2,1)S(1)} async-done(((bf16[16,5,2048]{2,1,0:T(8,128)(2,1)}), bf16[16,5,2048]{2,1,0:T(8,128)(2,1)S(1)}, u32[]{:S(2)}, u32[]{:S(2)}) %all-to-all-start.1) | async-done | bytes 327712 | tf_op jit(solution)/shard_map/while/body/eval_jaxpr/all_to_all | solution.py:56
  970.3 15.9 %all-to-all-done = bf16[16,5,2048]{2,1,0:T(8,128)(2,1)S(1)} async-done(((bf16[16,5,2048]{2,1,0:T(8,128)(2,1)}), bf16[16,5,2048]{2,1,0:T(8,128)(2,1)S(1)}, u32[]{:S(2)}, u32[]{:S(2)}) %all-to-all-start) | async-done | bytes 327712 | tf_op jit(solution)/shard_map/while/body/eval_jaxpr/all_to_all | solution.py:54
  998.8 16.1 %all-to-all-done.1 = bf16[16,5,2048]{2,1,0:T(8,128)(2,1)S(1)} async-done(((bf16[16,5,2048]{2,1,0:T(8,128)(2,1)}), bf16[16,5,2048]{2,1,0:T(8,128)(2,1)S(1)}, u32[]{:S(2)}, u32[]{:S(2)}) %all-to-all-start.1) | async-done | bytes 327712 | tf_op jit(solution)/shard_map/while/body/eval_jaxpr/all_to_all | solution.py:56
  1032.7 15.9 %all-to-all-done = bf16[16,5,2048]{2,1,0:T(8,128)(2,1)S(1)} async-done(((bf16[16,5,2048]{2,1,0:T(8,128)(2,1)}), bf16[16,5,2048]{2,1,0:T(8,128)(2,1)S(1)}, u32[]{:S(2)}, u32[]{:S(2)}) %all-to-all-start) | async-done | bytes 327712 | tf_op jit(solution)/shard_map/while/body/eval_jaxpr/all_to_all | solution.py:54
  1061.3 16.1 %all-to-all-done.1 = bf16[16,5,2048]{2,1,0:T(8,128)(2,1)S(1)} async-done(((bf16[16,5,2048]{2,1,0:T(8,128)(2,1)}), bf16[16,5,2048]{2,1,0:T(8,128)(2,1)S(1)}, u32[]{:S(2)}, u32[]{:S(2)}) %all-to-all-start.1) | async-done | bytes 327712 | tf_op jit(solution)/shard_map/while/body/eval_jaxpr/all_to_all | solution.py:56
  1095.1 15.9 %all-to-all-done = bf16[16,5,2048]{2,1,0:T(8,128)(2,1)S(1)} async-done(((bf16[16,5,2048]{2,1,0:T(8,128)(2,1)}), bf16[16,5,2048]{2,1,0:T(8,128)(2,1)S(1)}, u32[]{:S(2)}, u32[]{:S(2)}) %all-to-all-start) | async-done | bytes 327712 | tf_op jit(solution)/shard_map/while/body/eval_jaxpr/all_to_all | solution.py:54
  1123.7 16.1 %all-to-all-done.1 = bf16[16,5,2048]{2,1,0:T(8,128)(2,1)S(1)} async-done(((bf16[16,5,2048]{2,1,0:T(8,128)(2,1)}), bf16[16,5,2048]{2,1,0:T(8,128)(2,1)S(1)}, u32[]{:S(2)}, u32[]{:S(2)}) %all-to-all-start.1) | async-done | bytes 327712 | tf_op jit(solution)/shard_map/while/body/eval_jaxpr/all_to_all | solution.py:56
  1157.5 15.9 %all-to-all-done = bf16[16,5,2048]{2,1,0:T(8,128)(2,1)S(1)} async-done(((bf16[16,5,2048]{2,1,0:T(8,128)(2,1)}), bf16[16,5,2048]{2,1,0:T(8,128)(2,1)S(1)}, u32[]{:S(2)}, u32[]{:S(2)}) %all-to-all-start) | async-done | bytes 327712 | tf_op jit(solution)/shard_map/while/body/eval_jaxpr/all_to_all | solution.py:54
  1186.1 16.1 %all-to-all-done.1 = bf16[16,5,2048]{2,1,0:T(8,128)(2,1)S(1)} async-done(((bf16[16,5,2048]{2,1,0:T(8,128)(2,1)}), bf16[16,5,2048]{2,1,0:T(8,128)(2,1)S(1)}, u32[]{:S(2)}, u32[]{:S(2)}) %all-to-all-start.1) | async-done | bytes 327712 | tf_op jit(solution)/shard_map/while/body/eval_jaxpr/all_to_all | solution.py:56
  1219.9 15.9 %all-to-all-done = bf16[16,5,2048]{2,1,0:T(8,128)(2,1)S(1)} async-done(((bf16[16,5,2048]{2,1,0:T(8,128)(2,1)}), bf16[16,5,2048]{2,1,0:T(8,128)(2,1)S(1)}, u32[]{:S(2)}, u32[]{:S(2)}) %all-to-all-start) | async-done | bytes 327712 | tf_op jit(solution)/shard_map/while/body/eval_jaxpr/all_to_all | solution.py:54
  1248.5 16.1 %all-to-all-done.1 = bf16[16,5,2048]{2,1,0:T(8,128)(2,1)S(1)} async-done(((bf16[16,5,2048]{2,1,0:T(8,128)(2,1)}), bf16[16,5,2048]{2,1,0:T(8,128)(2,1)S(1)}, u32[]{:S(2)}, u32[]{:S(2)}) %all-to-all-start.1) | async-done | bytes 327712 | tf_op jit(solution)/shard_map/while/body/eval_jaxpr/all_to_all | solution.py:56
  1282.3 15.9 %all-to-all-done = bf16[16,5,2048]{2,1,0:T(8,128)(2,1)S(1)} async-done(((bf16[16,5,2048]{2,1,0:T(8,128)(2,1)}), bf16[16,5,2048]{2,1,0:T(8,128)(2,1)S(1)}, u32[]{:S(2)}, u32[]{:S(2)}) %all-to-all-start) | async-done | bytes 327712 | tf_op jit(solution)/shard_map/while/body/eval_jaxpr/all_to_all | solution.py:54
  1310.9 16.1 %all-to-all-done.1 = bf16[16,5,2048]{2,1,0:T(8,128)(2,1)S(1)} async-done(((bf16[16,5,2048]{2,1,0:T(8,128)(2,1)}), bf16[16,5,2048]{2,1,0:T(8,128)(2,1)S(1)}, u32[]{:S(2)}, u32[]{:S(2)}) %all-to-all-start.1) | async-done | bytes 327712 | tf_op jit(solution)/shard_map/while/body/eval_jaxpr/all_to_all | solution.py:56
  1344.7 15.9 %all-to-all-done = bf16[16,5,2048]{2,1,0:T(8,128)(2,1)S(1)} async-done(((bf16[16,5,2048]{2,1,0:T(8,128)(2,1)}), bf16[16,5,2048]{2,1,0:T(8,128)(2,1)S(1)}, u32[]{:S(2)}, u32[]{:S(2)}) %all-to-all-start) | async-done | bytes 327712 | tf_op jit(solution)/shard_map/while/body/eval_jaxpr/all_to_all | solution.py:54
  1373.3 16.1 %all-to-all-done.1 = bf16[16,5,2048]{2,1,0:T(8,128)(2,1)S(1)} async-done(((bf16[16,5,2048]{2,1,0:T(8,128)(2,1)}), bf16[16,5,2048]{2,1,0:T(8,128)(2,1)S(1)}, u32[]{:S(2)}, u32[]{:S(2)}) %all-to-all-start.1) | async-done | bytes 327712 | tf_op jit(solution)/shard_map/while/body/eval_jaxpr/all_to_all | solution.py:56
  (681 shorter events, 651.2 us)
Async XLA Ops:
  5.7 24.5 %all-to-all-start = ((bf16[16,5,2048]{2,1,0:T(8,128)(2,1)}), bf16[16,5,2048]{2,1,0:T(8,128)(2,1)S(1)}, u32[]{:S(2)}, u32[]{:S(2)}) async-start(bf16[16,5,2048]{2,1,0:T(8,128)(2,1)} %bitcast.98), calls=%async_computation | async-start | bytes 1048576 | tf_op jit(solution)/shard_map/while/body/eval_jaxpr/all_to_all | solution.py:54
  31.0 20.4 %all-to-all-start.1 = ((bf16[16,5,2048]{2,1,0:T(8,128)(2,1)}), bf16[16,5,2048]{2,1,0:T(8,128)(2,1)S(1)}, u32[]{:S(2)}, u32[]{:S(2)}) async-start(bf16[16,5,2048]{2,1,0:T(8,128)(2,1)} %get-tuple-element.654), calls=%async_computation.1 | async-start | bytes 1048576 | tf_op jit(solution)/shard_map/while/body/eval_jaxpr/all_to_all | solution.py:56
  63.3 19.6 %all-to-all-start = ((bf16[16,5,2048]{2,1,0:T(8,128)(2,1)}), bf16[16,5,2048]{2,1,0:T(8,128)(2,1)S(1)}, u32[]{:S(2)}, u32[]{:S(2)}) async-start(bf16[16,5,2048]{2,1,0:T(8,128)(2,1)} %bitcast.98), calls=%async_computation | async-start | bytes 1048576 | tf_op jit(solution)/shard_map/while/body/eval_jaxpr/all_to_all | solution.py:54
  83.8 20.4 %all-to-all-start.1 = ((bf16[16,5,2048]{2,1,0:T(8,128)(2,1)}), bf16[16,5,2048]{2,1,0:T(8,128)(2,1)S(1)}, u32[]{:S(2)}, u32[]{:S(2)}) async-start(bf16[16,5,2048]{2,1,0:T(8,128)(2,1)} %get-tuple-element.654), calls=%async_computation.1 | async-start | bytes 1048576 | tf_op jit(solution)/shard_map/while/body/eval_jaxpr/all_to_all | solution.py:56
  116.1 19.6 %all-to-all-start = ((bf16[16,5,2048]{2,1,0:T(8,128)(2,1)}), bf16[16,5,2048]{2,1,0:T(8,128)(2,1)S(1)}, u32[]{:S(2)}, u32[]{:S(2)}) async-start(bf16[16,5,2048]{2,1,0:T(8,128)(2,1)} %bitcast.98), calls=%async_computation | async-start | bytes 1048576 | tf_op jit(solution)/shard_map/while/body/eval_jaxpr/all_to_all | solution.py:54
  136.6 20.4 %all-to-all-start.1 = ((bf16[16,5,2048]{2,1,0:T(8,128)(2,1)}), bf16[16,5,2048]{2,1,0:T(8,128)(2,1)S(1)}, u32[]{:S(2)}, u32[]{:S(2)}) async-start(bf16[16,5,2048]{2,1,0:T(8,128)(2,1)} %get-tuple-element.654), calls=%async_computation.1 | async-start | bytes 1048576 | tf_op jit(solution)/shard_map/while/body/eval_jaxpr/all_to_all | solution.py:56
  168.9 19.6 %all-to-all-start = ((bf16[16,5,2048]{2,1,0:T(8,128)(2,1)}), bf16[16,5,2048]{2,1,0:T(8,128)(2,1)S(1)}, u32[]{:S(2)}, u32[]{:S(2)}) async-start(bf16[16,5,2048]{2,1,0:T(8,128)(2,1)} %bitcast.98), calls=%async_computation | async-start | bytes 1048576 | tf_op jit(solution)/shard_map/while/body/eval_jaxpr/all_to_all | solution.py:54
  189.3 20.4 %all-to-all-start.1 = ((bf16[16,5,2048]{2,1,0:T(8,128)(2,1)}), bf16[16,5,2048]{2,1,0:T(8,128)(2,1)S(1)}, u32[]{:S(2)}, u32[]{:S(2)}) async-start(bf16[16,5,2048]{2,1,0:T(8,128)(2,1)} %get-tuple-element.654), calls=%async_computation.1 | async-start | bytes 1048576 | tf_op jit(solution)/shard_map/while/body/eval_jaxpr/all_to_all | solution.py:56
  221.6 19.6 %all-to-all-start = ((bf16[16,5,2048]{2,1,0:T(8,128)(2,1)}), bf16[16,5,2048]{2,1,0:T(8,128)(2,1)S(1)}, u32[]{:S(2)}, u32[]{:S(2)}) async-start(bf16[16,5,2048]{2,1,0:T(8,128)(2,1)} %bitcast.98), calls=%async_computation | async-start | bytes 1048576 | tf_op jit(solution)/shard_map/while/body/eval_jaxpr/all_to_all | solution.py:54
  242.1 20.4 %all-to-all-start.1 = ((bf16[16,5,2048]{2,1,0:T(8,128)(2,1)}), bf16[16,5,2048]{2,1,0:T(8,128)(2,1)S(1)}, u32[]{:S(2)}, u32[]{:S(2)}) async-start(bf16[16,5,2048]{2,1,0:T(8,128)(2,1)} %get-tuple-element.654), calls=%async_computation.1 | async-start | bytes 1048576 | tf_op jit(solution)/shard_map/while/body/eval_jaxpr/all_to_all | solution.py:56
  274.5 20.2 %all-to-all-start = ((bf16[16,5,2048]{2,1,0:T(8,128)(2,1)}), bf16[16,5,2048]{2,1,0:T(8,128)(2,1)S(1)}, u32[]{:S(2)}, u32[]{:S(2)}) async-start(bf16[16,5,2048]{2,1,0:T(8,128)(2,1)} %bitcast.98), calls=%async_computation | async-start | bytes 1048576 | tf_op jit(solution)/shard_map/while/body/eval_jaxpr/all_to_all | solution.py:54
  295.5 20.4 %all-to-all-start.1 = ((bf16[16,5,2048]{2,1,0:T(8,128)(2,1)}), bf16[16,5,2048]{2,1,0:T(8,128)(2,1)S(1)}, u32[]{:S(2)}, u32[]{:S(2)}) async-start(bf16[16,5,2048]{2,1,0:T(8,128)(2,1)} %get-tuple-element.654), calls=%async_computation.1 | async-start | bytes 1048576 | tf_op jit(solution)/shard_map/while/body/eval_jaxpr/all_to_all | solution.py:56
  329.4 20.2 %all-to-all-start = ((bf16[16,5,2048]{2,1,0:T(8,128)(2,1)}), bf16[16,5,2048]{2,1,0:T(8,128)(2,1)S(1)}, u32[]{:S(2)}, u32[]{:S(2)}) async-start(bf16[16,5,2048]{2,1,0:T(8,128)(2,1)} %bitcast.98), calls=%async_computation | async-start | bytes 1048576 | tf_op jit(solution)/shard_map/while/body/eval_jaxpr/all_to_all | solution.py:54
  350.4 20.4 %all-to-all-start.1 = ((bf16[16,5,2048]{2,1,0:T(8,128)(2,1)}), bf16[16,5,2048]{2,1,0:T(8,128)(2,1)S(1)}, u32[]{:S(2)}, u32[]{:S(2)}) async-start(bf16[16,5,2048]{2,1,0:T(8,128)(2,1)} %get-tuple-element.654), calls=%async_computation.1 | async-start | bytes 1048576 | tf_op jit(solution)/shard_map/while/body/eval_jaxpr/all_to_all | solution.py:56
  384.3 20.2 %all-to-all-start = ((bf16[16,5,2048]{2,1,0:T(8,128)(2,1)}), bf16[16,5,2048]{2,1,0:T(8,128)(2,1)S(1)}, u32[]{:S(2)}, u32[]{:S(2)}) async-start(bf16[16,5,2048]{2,1,0:T(8,128)(2,1)} %bitcast.98), calls=%async_computation | async-start | bytes 1048576 | tf_op jit(solution)/shard_map/while/body/eval_jaxpr/all_to_all | solution.py:54
  405.3 20.4 %all-to-all-start.1 = ((bf16[16,5,2048]{2,1,0:T(8,128)(2,1)}), bf16[16,5,2048]{2,1,0:T(8,128)(2,1)S(1)}, u32[]{:S(2)}, u32[]{:S(2)}) async-start(bf16[16,5,2048]{2,1,0:T(8,128)(2,1)} %get-tuple-element.654), calls=%async_computation.1 | async-start | bytes 1048576 | tf_op jit(solution)/shard_map/while/body/eval_jaxpr/all_to_all | solution.py:56
  439.1 20.2 %all-to-all-start = ((bf16[16,5,2048]{2,1,0:T(8,128)(2,1)}), bf16[16,5,2048]{2,1,0:T(8,128)(2,1)S(1)}, u32[]{:S(2)}, u32[]{:S(2)}) async-start(bf16[16,5,2048]{2,1,0:T(8,128)(2,1)} %bitcast.98), calls=%async_computation | async-start | bytes 1048576 | tf_op jit(solution)/shard_map/while/body/eval_jaxpr/all_to_all | solution.py:54
  460.2 20.4 %all-to-all-start.1 = ((bf16[16,5,2048]{2,1,0:T(8,128)(2,1)}), bf16[16,5,2048]{2,1,0:T(8,128)(2,1)S(1)}, u32[]{:S(2)}, u32[]{:S(2)}) async-start(bf16[16,5,2048]{2,1,0:T(8,128)(2,1)} %get-tuple-element.654), calls=%async_computation.1 | async-start | bytes 1048576 | tf_op jit(solution)/shard_map/while/body/eval_jaxpr/all_to_all | solution.py:56
  494.0 20.2 %all-to-all-start = ((bf16[16,5,2048]{2,1,0:T(8,128)(2,1)}), bf16[16,5,2048]{2,1,0:T(8,128)(2,1)S(1)}, u32[]{:S(2)}, u32[]{:S(2)}) async-start(bf16[16,5,2048]{2,1,0:T(8,128)(2,1)} %bitcast.98), calls=%async_computation | async-start | bytes 1048576 | tf_op jit(solution)/shard_map/while/body/eval_jaxpr/all_to_all | solution.py:54
  515.0 20.4 %all-to-all-start.1 = ((bf16[16,5,2048]{2,1,0:T(8,128)(2,1)}), bf16[16,5,2048]{2,1,0:T(8,128)(2,1)S(1)}, u32[]{:S(2)}, u32[]{:S(2)}) async-start(bf16[16,5,2048]{2,1,0:T(8,128)(2,1)} %get-tuple-element.654), calls=%async_computation.1 | async-start | bytes 1048576 | tf_op jit(solution)/shard_map/while/body/eval_jaxpr/all_to_all | solution.py:56
  548.9 20.2 %all-to-all-start = ((bf16[16,5,2048]{2,1,0:T(8,128)(2,1)}), bf16[16,5,2048]{2,1,0:T(8,128)(2,1)S(1)}, u32[]{:S(2)}, u32[]{:S(2)}) async-start(bf16[16,5,2048]{2,1,0:T(8,128)(2,1)} %bitcast.98), calls=%async_computation | async-start | bytes 1048576 | tf_op jit(solution)/shard_map/while/body/eval_jaxpr/all_to_all | solution.py:54
  569.9 20.4 %all-to-all-start.1 = ((bf16[16,5,2048]{2,1,0:T(8,128)(2,1)}), bf16[16,5,2048]{2,1,0:T(8,128)(2,1)S(1)}, u32[]{:S(2)}, u32[]{:S(2)}) async-start(bf16[16,5,2048]{2,1,0:T(8,128)(2,1)} %get-tuple-element.654), calls=%async_computation.1 | async-start | bytes 1048576 | tf_op jit(solution)/shard_map/while/body/eval_jaxpr/all_to_all | solution.py:56
  603.8 20.2 %all-to-all-start = ((bf16[16,5,2048]{2,1,0:T(8,128)(2,1)}), bf16[16,5,2048]{2,1,0:T(8,128)(2,1)S(1)}, u32[]{:S(2)}, u32[]{:S(2)}) async-start(bf16[16,5,2048]{2,1,0:T(8,128)(2,1)} %bitcast.98), calls=%async_computation | async-start | bytes 1048576 | tf_op jit(solution)/shard_map/while/body/eval_jaxpr/all_to_all | solution.py:54
  624.8 20.4 %all-to-all-start.1 = ((bf16[16,5,2048]{2,1,0:T(8,128)(2,1)}), bf16[16,5,2048]{2,1,0:T(8,128)(2,1)S(1)}, u32[]{:S(2)}, u32[]{:S(2)}) async-start(bf16[16,5,2048]{2,1,0:T(8,128)(2,1)} %get-tuple-element.654), calls=%async_computation.1 | async-start | bytes 1048576 | tf_op jit(solution)/shard_map/while/body/eval_jaxpr/all_to_all | solution.py:56
  658.6 20.2 %all-to-all-start = ((bf16[16,5,2048]{2,1,0:T(8,128)(2,1)}), bf16[16,5,2048]{2,1,0:T(8,128)(2,1)S(1)}, u32[]{:S(2)}, u32[]{:S(2)}) async-start(bf16[16,5,2048]{2,1,0:T(8,128)(2,1)} %bitcast.98), calls=%async_computation | async-start | bytes 1048576 | tf_op jit(solution)/shard_map/while/body/eval_jaxpr/all_to_all | solution.py:54
  679.7 20.4 %all-to-all-start.1 = ((bf16[16,5,2048]{2,1,0:T(8,128)(2,1)}), bf16[16,5,2048]{2,1,0:T(8,128)(2,1)S(1)}, u32[]{:S(2)}, u32[]{:S(2)}) async-start(bf16[16,5,2048]{2,1,0:T(8,128)(2,1)} %get-tuple-element.654), calls=%async_computation.1 | async-start | bytes 1048576 | tf_op jit(solution)/shard_map/while/body/eval_jaxpr/all_to_all | solution.py:56
  713.5 20.2 %all-to-all-start = ((bf16[16,5,2048]{2,1,0:T(8,128)(2,1)}), bf16[16,5,2048]{2,1,0:T(8,128)(2,1)S(1)}, u32[]{:S(2)}, u32[]{:S(2)}) async-start(bf16[16,5,2048]{2,1,0:T(8,128)(2,1)} %bitcast.98), calls=%async_computation | async-start | bytes 1048576 | tf_op jit(solution)/shard_map/while/body/eval_jaxpr/all_to_all | solution.py:54
  734.5 20.4 %all-to-all-start.1 = ((bf16[16,5,2048]{2,1,0:T(8,128)(2,1)}), bf16[16,5,2048]{2,1,0:T(8,128)(2,1)S(1)}, u32[]{:S(2)}, u32[]{:S(2)}) async-start(bf16[16,5,2048]{2,1,0:T(8,128)(2,1)} %get-tuple-element.654), calls=%async_computation.1 | async-start | bytes 1048576 | tf_op jit(solution)/shard_map/while/body/eval_jaxpr/all_to_all | solution.py:56
  768.4 20.2 %all-to-all-start = ((bf16[16,5,2048]{2,1,0:T(8,128)(2,1)}), bf16[16,5,2048]{2,1,0:T(8,128)(2,1)S(1)}, u32[]{:S(2)}, u32[]{:S(2)}) async-start(bf16[16,5,2048]{2,1,0:T(8,128)(2,1)} %bitcast.98), calls=%async_computation | async-start | bytes 1048576 | tf_op jit(solution)/shard_map/while/body/eval_jaxpr/all_to_all | solution.py:54
  789.4 20.4 %all-to-all-start.1 = ((bf16[16,5,2048]{2,1,0:T(8,128)(2,1)}), bf16[16,5,2048]{2,1,0:T(8,128)(2,1)S(1)}, u32[]{:S(2)}, u32[]{:S(2)}) async-start(bf16[16,5,2048]{2,1,0:T(8,128)(2,1)} %get-tuple-element.654), calls=%async_computation.1 | async-start | bytes 1048576 | tf_op jit(solution)/shard_map/while/body/eval_jaxpr/all_to_all | solution.py:56
  811.3 88.9 %collective-permute-start = (bf16[3,8,2048]{2,1,0:T(8,128)(2,1)S(1)}, bf16[3,8,2048]{2,1,0:T(8,128)(2,1)S(1)}, u32[]{:S(2)}, u32[]{:S(2)}) collective-permute-start(bf16[3,8,2048]{2,1,0:T(8,128)(2,1)S(1)} %maximum_select_fusion.2), channel_id=1, source_target_pairs={{0,16},{16,32},{32,48},{48,64},{64,80},{80,96},{96,112},{112,128},... | collective-permute-start | bytes 294920 | tf_op jit(solution)/shard_map/while/body/eval_jaxpr/ppermute | solution.py:16
  903.6 20.2 %all-to-all-start = ((bf16[16,5,2048]{2,1,0:T(8,128)(2,1)}), bf16[16,5,2048]{2,1,0:T(8,128)(2,1)S(1)}, u32[]{:S(2)}, u32[]{:S(2)}) async-start(bf16[16,5,2048]{2,1,0:T(8,128)(2,1)} %bitcast.98), calls=%async_computation | async-start | bytes 1048576 | tf_op jit(solution)/shard_map/while/body/eval_jaxpr/all_to_all | solution.py:54
  932.1 20.4 %all-to-all-start.1 = ((bf16[16,5,2048]{2,1,0:T(8,128)(2,1)}), bf16[16,5,2048]{2,1,0:T(8,128)(2,1)S(1)}, u32[]{:S(2)}, u32[]{:S(2)}) async-start(bf16[16,5,2048]{2,1,0:T(8,128)(2,1)} %get-tuple-element.654), calls=%async_computation.1 | async-start | bytes 1048576 | tf_op jit(solution)/shard_map/while/body/eval_jaxpr/all_to_all | solution.py:56
  954.0 8.6 collective-permute-start
  966.0 20.2 %all-to-all-start = ((bf16[16,5,2048]{2,1,0:T(8,128)(2,1)}), bf16[16,5,2048]{2,1,0:T(8,128)(2,1)S(1)}, u32[]{:S(2)}, u32[]{:S(2)}) async-start(bf16[16,5,2048]{2,1,0:T(8,128)(2,1)} %bitcast.98), calls=%async_computation | async-start | bytes 1048576 | tf_op jit(solution)/shard_map/while/body/eval_jaxpr/all_to_all | solution.py:54
  994.5 20.4 %all-to-all-start.1 = ((bf16[16,5,2048]{2,1,0:T(8,128)(2,1)}), bf16[16,5,2048]{2,1,0:T(8,128)(2,1)S(1)}, u32[]{:S(2)}, u32[]{:S(2)}) async-start(bf16[16,5,2048]{2,1,0:T(8,128)(2,1)} %get-tuple-element.654), calls=%async_computation.1 | async-start | bytes 1048576 | tf_op jit(solution)/shard_map/while/body/eval_jaxpr/all_to_all | solution.py:56
  1028.4 20.2 %all-to-all-start = ((bf16[16,5,2048]{2,1,0:T(8,128)(2,1)}), bf16[16,5,2048]{2,1,0:T(8,128)(2,1)S(1)}, u32[]{:S(2)}, u32[]{:S(2)}) async-start(bf16[16,5,2048]{2,1,0:T(8,128)(2,1)} %bitcast.98), calls=%async_computation | async-start | bytes 1048576 | tf_op jit(solution)/shard_map/while/body/eval_jaxpr/all_to_all | solution.py:54
  1057.0 20.4 %all-to-all-start.1 = ((bf16[16,5,2048]{2,1,0:T(8,128)(2,1)}), bf16[16,5,2048]{2,1,0:T(8,128)(2,1)S(1)}, u32[]{:S(2)}, u32[]{:S(2)}) async-start(bf16[16,5,2048]{2,1,0:T(8,128)(2,1)} %get-tuple-element.654), calls=%async_computation.1 | async-start | bytes 1048576 | tf_op jit(solution)/shard_map/while/body/eval_jaxpr/all_to_all | solution.py:56
  1090.8 20.2 %all-to-all-start = ((bf16[16,5,2048]{2,1,0:T(8,128)(2,1)}), bf16[16,5,2048]{2,1,0:T(8,128)(2,1)S(1)}, u32[]{:S(2)}, u32[]{:S(2)}) async-start(bf16[16,5,2048]{2,1,0:T(8,128)(2,1)} %bitcast.98), calls=%async_computation | async-start | bytes 1048576 | tf_op jit(solution)/shard_map/while/body/eval_jaxpr/all_to_all | solution.py:54
  1119.4 20.4 %all-to-all-start.1 = ((bf16[16,5,2048]{2,1,0:T(8,128)(2,1)}), bf16[16,5,2048]{2,1,0:T(8,128)(2,1)S(1)}, u32[]{:S(2)}, u32[]{:S(2)}) async-start(bf16[16,5,2048]{2,1,0:T(8,128)(2,1)} %get-tuple-element.654), calls=%async_computation.1 | async-start | bytes 1048576 | tf_op jit(solution)/shard_map/while/body/eval_jaxpr/all_to_all | solution.py:56
  1153.2 20.2 %all-to-all-start = ((bf16[16,5,2048]{2,1,0:T(8,128)(2,1)}), bf16[16,5,2048]{2,1,0:T(8,128)(2,1)S(1)}, u32[]{:S(2)}, u32[]{:S(2)}) async-start(bf16[16,5,2048]{2,1,0:T(8,128)(2,1)} %bitcast.98), calls=%async_computation | async-start | bytes 1048576 | tf_op jit(solution)/shard_map/while/body/eval_jaxpr/all_to_all | solution.py:54
  1181.8 20.4 %all-to-all-start.1 = ((bf16[16,5,2048]{2,1,0:T(8,128)(2,1)}), bf16[16,5,2048]{2,1,0:T(8,128)(2,1)S(1)}, u32[]{:S(2)}, u32[]{:S(2)}) async-start(bf16[16,5,2048]{2,1,0:T(8,128)(2,1)} %get-tuple-element.654), calls=%async_computation.1 | async-start | bytes 1048576 | tf_op jit(solution)/shard_map/while/body/eval_jaxpr/all_to_all | solution.py:56
  1215.6 20.2 %all-to-all-start = ((bf16[16,5,2048]{2,1,0:T(8,128)(2,1)}), bf16[16,5,2048]{2,1,0:T(8,128)(2,1)S(1)}, u32[]{:S(2)}, u32[]{:S(2)}) async-start(bf16[16,5,2048]{2,1,0:T(8,128)(2,1)} %bitcast.98), calls=%async_computation | async-start | bytes 1048576 | tf_op jit(solution)/shard_map/while/body/eval_jaxpr/all_to_all | solution.py:54
  1244.2 20.4 %all-to-all-start.1 = ((bf16[16,5,2048]{2,1,0:T(8,128)(2,1)}), bf16[16,5,2048]{2,1,0:T(8,128)(2,1)S(1)}, u32[]{:S(2)}, u32[]{:S(2)}) async-start(bf16[16,5,2048]{2,1,0:T(8,128)(2,1)} %get-tuple-element.654), calls=%async_computation.1 | async-start | bytes 1048576 | tf_op jit(solution)/shard_map/while/body/eval_jaxpr/all_to_all | solution.py:56
  1278.0 20.2 %all-to-all-start = ((bf16[16,5,2048]{2,1,0:T(8,128)(2,1)}), bf16[16,5,2048]{2,1,0:T(8,128)(2,1)S(1)}, u32[]{:S(2)}, u32[]{:S(2)}) async-start(bf16[16,5,2048]{2,1,0:T(8,128)(2,1)} %bitcast.98), calls=%async_computation | async-start | bytes 1048576 | tf_op jit(solution)/shard_map/while/body/eval_jaxpr/all_to_all | solution.py:54
  1306.6 20.4 %all-to-all-start.1 = ((bf16[16,5,2048]{2,1,0:T(8,128)(2,1)}), bf16[16,5,2048]{2,1,0:T(8,128)(2,1)S(1)}, u32[]{:S(2)}, u32[]{:S(2)}) async-start(bf16[16,5,2048]{2,1,0:T(8,128)(2,1)} %get-tuple-element.654), calls=%async_computation.1 | async-start | bytes 1048576 | tf_op jit(solution)/shard_map/while/body/eval_jaxpr/all_to_all | solution.py:56
  1340.4 20.2 %all-to-all-start = ((bf16[16,5,2048]{2,1,0:T(8,128)(2,1)}), bf16[16,5,2048]{2,1,0:T(8,128)(2,1)S(1)}, u32[]{:S(2)}, u32[]{:S(2)}) async-start(bf16[16,5,2048]{2,1,0:T(8,128)(2,1)} %bitcast.98), calls=%async_computation | async-start | bytes 1048576 | tf_op jit(solution)/shard_map/while/body/eval_jaxpr/all_to_all | solution.py:54
  1369.0 20.4 %all-to-all-start.1 = ((bf16[16,5,2048]{2,1,0:T(8,128)(2,1)}), bf16[16,5,2048]{2,1,0:T(8,128)(2,1)S(1)}, u32[]{:S(2)}, u32[]{:S(2)}) async-start(bf16[16,5,2048]{2,1,0:T(8,128)(2,1)} %get-tuple-element.654), calls=%async_computation.1 | async-start | bytes 1048576 | tf_op jit(solution)/shard_map/while/body/eval_jaxpr/all_to_all | solution.py:56
  (23 other events, 174.9 us)
where the time goes:
time: 1410 us; the launch traced here: 1400 us
  waiting for transfers between devices  975 us (69%)
  starting transfers between devices  227 us (16%)
  local copies, waits for them, and re-layouts  72.2 us (5%)
  other arithmetic  62.3 us (4%)
  matrix products  58.3 us (4%)
    all_to_all x23, waiting for transfers between devices, run_experts(): lax.all_to_all(computed, 'expert', split_axis=0, concat_axis=0, tiled=True)  370 us
    all_to_all x23, waiting for transfers between devices, run_experts(): lax.all_to_all(outgoing, 'expert', split_axis=0, concat_axis=0, tiled=True)  366 us
    ppermute x23, waiting for transfers between devices, shifted(): return lax.ppermute(value, axis, pairs)  240 us
    all_to_all x23, starting transfers between devices, run_experts(): lax.all_to_all(outgoing, 'expert', split_axis=0, concat_axis=0, tiled=True)  99.3 us
    all_to_all x23, starting transfers between devices, run_experts(): lax.all_to_all(computed, 'expert', split_axis=0, concat_axis=0, tiled=True)  97.6 us
    dot_general x8, matrix products, expert_rows(): jnp.dot(hidden, down_mat, preferred_element_type=jnp.float32)  36.4 us
    ppermute x23, starting transfers between devices, shifted(): return lax.ppermute(value, axis, pairs)  29.7 us
  transfers between devices with their start and end apart: 69, of which 69 were waited for; matrix products, arithmetic and copies ran while one was open for 0% of the time, Pallas kernels for 0%

commit v1 on v0

v1 whole, which is shorter than its diff:
```python
import functools

import jax
import jax.numpy as jnp
from jax import lax
from jax.experimental import pallas as pl
from jax.experimental.pallas import tpu as pltpu
from jax.sharding import PartitionSpec as P

EXPERTS = 4
LANES = 128
LAG = 1
MESH = pl.DeviceIdType.MESH
BF16 = jnp.bfloat16
F32 = jnp.float32


def kernel(
    dims,
    dtab,
    ctab,
    wtab,
    tok,
    gain,
    wg_hbm,
    wu_hbm,
    wd_hbm,
    out,
    wgu,
    wd,
    arows,
    rrows,
    disp,
    xbuf,
    normed,
    stage,
    psend,
    precv,
    rsend,
    tall,
    xmat,
    gu,
    hid,
    summed,
    w_sem,
    disp_sem,
    init_sem,
    a_sem,
    relay_send,
    relay_recv,
    pair_send,
    pair_recv,
    rs_send,
    rs_recv,
    x_send,
    x_recv,
    st_send,
    st_recv,
):
    micros, depth, layers, zsize, cap, sub = dims
    toks = tok.shape[1]
    group = zsize * cap
    ff = wg_hbm.shape[2]
    sec = lax.axis_index("section")
    g = lax.axis_index("expert")
    layer = sec // 2
    col = sec % 2
    z = g // 2
    core = g % 2
    partner = 2 * z + (1 - core)
    owner = col == core
    slots = EXPERTS * cap

    def load_weights():
        return (
            pltpu.make_async_copy(wg_hbm.at[0], wgu.at[:, pl.ds(0, ff)], w_sem.at[0]),
            pltpu.make_async_copy(wu_hbm.at[0], wgu.at[:, pl.ds(ff, ff)], w_sem.at[1]),
            pltpu.make_async_copy(wd_hbm.at[0], wd, w_sem.at[2]),
        )

    for copy in load_weights():
        copy.start()

    def taken(ref, sem):
        pltpu.make_async_copy(ref, ref, sem).wait()

    def normalize(rows, gain_row):
        wide = rows.astype(F32)
        square = jnp.sum(wide * wide, axis=2, keepdims=True)
        square = jnp.sum(square, axis=1, keepdims=True)
        scale = lax.rsqrt(square * (1.0 / depth) + 1e-05)
        normed[...] = (wide * scale * gain_row[None]).astype(BF16)

    def spread(m, table, slot, send_sem, next_layer, may_self):
        for q in range(slots):
            disp[slot, q] = normed[dtab[table + m * slots + q]]

        def one(i, carry):
            to_col = i // zsize
            to_z = (z + i) % zsize
            expert = 2 * to_col + to_z // (zsize // 2)
            src = disp.at[slot, pl.ds(expert * cap, cap)]
            dst = arows.at[m, core, pl.ds(z * cap, cap)]

            def remote():
                pltpu.make_async_remote_copy(
                    src_ref=src,
                    dst_ref=dst,
                    send_sem=send_sem.at[m],
                    recv_sem=a_sem.at[m],
                    device_id=(2 * next_layer + to_col, 2 * to_z + core),
                    device_id_type=MESH,
                ).start()

            if may_self:
                here = (to_col == col) & (to_z == z)

                @pl.when(here)
                def _():
                    pltpu.make_async_copy(src, dst, a_sem.at[m]).start()

                @pl.when(jnp.logical_not(here))
                def _():
                    remote()
            else:
                remote()
            return carry

        lax.fori_loop(0, 2 * zsize, one, 0)

    def enter(m):
        normalize(tok[m], gain[0])
        spread(m, micros * slots, micros + m, init_sem, 0, True)

    def x_copy(m):
        return pltpu.make_async_remote_copy(
            src_ref=stage.at[m, 1],
            dst_ref=xbuf.at[m],
            send_sem=x_send.at[m],
            recv_sem=x_recv.at[m],
            device_id=(sec + 2, g),
            device_id_type=MESH,
        )

    def state_copy(m):
        return pltpu.make_async_remote_copy(
            src_ref=stage.at[m, 1 - core],
            dst_ref=out.at[m],
            send_sem=st_send.at[m],
            recv_sem=st_recv.at[m],
            device_id=(2 * layer + 1 - core, g),
            device_id_type=MESH,
        )

    def relay_copy(m):
        return pltpu.make_async_remote_copy(
            src_ref=arows.at[m, core],
            dst_ref=arows.at[m, core],
            send_sem=relay_send.at[m],
            recv_sem=relay_recv.at[m],
            device_id=(sec, partner),
            device_id_type=MESH,
        )

    def pair_copy(m):
        return pltpu.make_async_remote_copy(
            src_ref=psend.at[m],
            dst_ref=precv.at[m],
            send_sem=pair_send.at[m],
            recv_sem=pair_recv.at[m],
            device_id=(sec, partner),
            device_id_type=MESH,
        )

    def experts(m):
        taken(arows.at[m, core], a_sem.at[m])
        relay_copy(m).start()

        @pl.when(m == 0)
        def _():
            for copy in load_weights():
                copy.wait()

        taken(arows.at[m, 1 - core], relay_recv.at[m])
        tall[...] = arows[m].reshape(2 * group * sub, LANES).astype(F32)
        for k in range(sub):
            xmat[:, k * LANES : (k + 1) * LANES] = tall[
                pl.ds(k, 2 * group, stride=sub), :
            ].astype(BF16)
        width = 2 * LANES
        for n in range(2 * ff // width):
            cols = slice(n * width, (n + 1) * width)
            gu[:, cols] = jnp.dot(xmat[...], wgu[:, cols], preferred_element_type=F32)
        gate = gu[:, :ff]
        hid[...] = (gate / (1.0 + jnp.exp(-gate)) * gu[:, ff:]).astype(BF16)
        for n in range(depth // width):
            part = jnp.dot(
                hid[...], wd[:, n * width : (n + 1) * width], preferred_element_type=F32
            )
            for k in range(2):
                tall[pl.ds(2 * n + k, 2 * group, stride=sub), :] = part[
                    :, k * LANES : (k + 1) * LANES
                ]
        away = pl.multiple_of((1 - core) * group * sub, group * sub)
        home = pl.multiple_of(core * group * sub, group * sub)
        psend[m] = tall[pl.ds(away, group * sub), :].astype(BF16).reshape(group, sub, LANES)
        pair_copy(m).start()
        taken(precv.at[m], pair_recv.at[m])
        mine = tall[pl.ds(home, group * sub), :].reshape(group, sub, LANES)
        rsend[m] = (mine + precv[m].astype(F32)).astype(BF16)

        def one(i, carry):
            to_z = (z + i) % zsize
            src = rsend.at[m, pl.ds(to_z * cap, cap)]
            dst = rrows.at[m, pl.ds((col * zsize + z) * cap, cap)]
            here = owner & (to_z == z)

            @pl.when(here)
            def _():
                pltpu.make_async_copy(src, dst, rs_recv.at[m]).start()

            @pl.when(jnp.logical_not(here))
            def _():
                pltpu.make_async_remote_copy(
                    src_ref=src,
                    dst_ref=dst,
                    send_sem=rs_send.at[m],
                    recv_sem=rs_recv.at[m],
                    device_id=(2 * layer + core, 2 * to_z + core),
                    device_id_type=MESH,
                ).start()

            return carry

        lax.fori_loop(0, zsize, one, 0)

    def combine(m):
        taken(rrows.at[m], rs_recv.at[m])

        @pl.when(layer > 0)
        def _():
            taken(xbuf.at[m], x_recv.at[m])

        for e in range(EXPERTS):
            first = e * (zsize // 2) * cap
            total = rrows[m, first : first + cap].astype(F32)
            for b in range(1, zsize // 2):
                start = first + b * cap
                total = total + rrows[m, start : start + cap].astype(F32)
            summed[e * cap : (e + 1) * cap] = total.astype(BF16).astype(F32)
        for t in range(toks):
            wide = xbuf[m, t].astype(F32)
            at = (m * toks + t) * 2
            chosen = [summed[ctab[at + k]] for k in range(2)]
            far = micros * toks * 2
            half = wide + wtab[at] * chosen[0] + wtab[at + 1] * chosen[1]
            full = half + wtab[far + at] * chosen[0] + wtab[far + at + 1] * chosen[1]
            stage[m, 0, t] = half.astype(BF16)
            stage[m, 1, t] = full.astype(BF16)

        @pl.when(layer < layers - 1)
        def _():
            normalize(stage[m, 1], gain[jnp.minimum(layer + 1, layers - 1)])
            spread(m, 0, m, disp_sem, layer + 1, False)
            x_copy(m).start()

        state_copy(m).start()
        out[m] = stage[m, core]

    entering = owner & (layer == 0)

    @pl.when(entering)
    def _():
        xbuf[...] = tok[...]
        enter(0)

    def step(i, carry):
        @pl.when(entering & (i + 1 < micros))
        def _():
            enter(i + 1)

        @pl.when(i < micros)
        def _():
            experts(i)

        @pl.when(owner & (i >= LAG))
        def _():
            combine(i - LAG)

        return carry

    lax.fori_loop(0, micros + LAG, step, 0)

    def finish(m, carry):
        relay_copy(m).wait_send()
        pair_copy(m).wait_send()

        @pl.when(owner)
        def _():
            taken(rsend.at[m, pl.ds(0, group - cap)], rs_send.at[m])
            state_copy(m).wait_send()

            @pl.when(layer < layers - 1)
            def _():
                taken(rrows.at[m], disp_sem.at[m])
                x_copy(m).wait_send()

        @pl.when(jnp.logical_not(owner))
        def _():
            taken(rsend.at[m], rs_send.at[m])
            state_copy(m).wait_recv()

        @pl.when(entering)
        def _():
            taken(rrows.at[m, pl.ds(0, 2 * group - cap)], init_sem.at[m])

        return carry

    lax.fori_loop(0, micros, finish, 0)


def on_device(tokens, norm_gain, w_gate, w_up, w_down, expert_ids, slot_ids, dropped, gate_weights):
    micros, toks, depth = tokens.shape
    layers = norm_gain.shape[0]
    ff = w_gate.shape[2]
    zsize = lax.axis_size("expert") // 2
    cap = 5 * toks // (2 * EXPERTS)
    sub = depth // LANES
    group = zsize * cap
    layer = lax.axis_index("section") // 2
    slots = EXPERTS * cap

    def at_layer(value, index):
        return lax.dynamic_index_in_dim(value, index, 0, keepdims=False)

    key_all = jnp.where(dropped == 0, expert_ids * cap + slot_ids, -1)
    keys = jnp.stack([at_layer(key_all, jnp.minimum(layer + 1, layers - 1)), key_all[0]])
    token_at = jnp.arange(toks, dtype=jnp.int32)[:, None, None]
    hits = keys[..., None] == jnp.arange(slots, dtype=jnp.int32)
    dtab = jnp.sum(jnp.where(hits, token_at, 0), axis=(2, 3)).reshape(-1)
    ids = at_layer(expert_ids, layer)
    ctab = (ids * cap + at_layer(slot_ids, layer)).reshape(-1)
    weigh = jnp.where(at_layer(dropped, layer) == 0, at_layer(gate_weights, layer), 0.0)
    first = ids < EXPERTS // 2
    wtab = jnp.stack([jnp.where(first, weigh, 0.0), jnp.where(first, 0.0, weigh)]).reshape(-1)

    smem = pl.BlockSpec(memory_space=pltpu.SMEM)
    vmem = pl.BlockSpec(memory_space=pltpu.VMEM)
    hbm = pl.BlockSpec(memory_space=pl.ANY)
    tile = (sub, LANES)
    dma = pltpu.SemaphoreType.DMA
    states = pl.pallas_call(
        functools.partial(kernel, (micros, depth, layers, zsize, cap, sub)),
        out_shape=jax.ShapeDtypeStruct((micros, toks) + tile, BF16),
        in_specs=[smem, smem, smem, vmem, vmem, hbm, hbm, hbm],
        out_specs=vmem,
        scratch_shapes=[
            pltpu.VMEM((depth, 2 * ff), BF16),
            pltpu.VMEM((ff, depth), BF16),
            pltpu.VMEM((micros, 2, group) + tile, BF16),
            pltpu.VMEM((micros, 2 * group) + tile, BF16),
            pltpu.VMEM((2 * micros, slots) + tile, BF16),
            pltpu.VMEM((micros, toks) + tile, BF16),
            pltpu.VMEM((toks,) + tile, BF16),
            pltpu.VMEM((micros, 2, toks) + tile, BF16),
            pltpu.VMEM((micros, group) + tile, BF16),
            pltpu.VMEM((micros, group) + tile, BF16),
            pltpu.VMEM((micros, group) + tile, BF16),
            pltpu.VMEM((2 * group * sub, LANES), F32),
            pltpu.VMEM((2 * group, depth), BF16),
            pltpu.VMEM((2 * group, 2 * ff), F32),
            pltpu.VMEM((2 * group, ff), BF16),
            pltpu.VMEM((slots,) + tile, F32),
            dma((3,)),
        ]
        + [dma((micros,))] * 13,
        compiler_params=pltpu.CompilerParams(
            has_side_effects=True, vmem_limit_bytes=60 * 1024 * 1024
        ),
    )(
        dtab,
        ctab,
        wtab,
        tokens.reshape((micros, toks) + tile),
        norm_gain.reshape((layers,) + tile),
        w_gate,
        w_up,
        w_down,
    )
    return states.reshape(1, micros, toks, depth)


def solution(mesh):
    return jax.shard_map(
        on_device,
        mesh=mesh,
        in_specs=(
            P(None, "expert", None),
            P(),
            P("section", None, "expert"),
            P("section", None, "expert"),
            P("section", "expert", None),
            P(None, None, "expert", None),
            P(None, None, "expert", None),
            P(None, None, "expert", None),
            P(None, None, "expert", None),
        ),
        out_specs=P("section", None, "expert", None),
        check_vma=False,
    )
```

time: 1410 us -> 289 us (0.20)
  waiting for transfers between devices: 975 us -> 0 us
  Pallas kernels: 0 us -> 277 us
  starting transfers between devices: 227 us -> 0 us
  local copies, waits for them, and re-layouts: 72.2 us -> 7.31 us
  other arithmetic: 62.3 us -> 2.56 us
  matrix products: 58.3 us -> 0 us
    all_to_all x46 -> x0, waiting for transfers between devices: 736 us -> none  [the longest x23 370 us: run_experts(): lax.all_to_all(computed, 'expert', split_axis=0, concat_axis=0, tiled=True)]
    pallas_call x0 -> x1, Pallas kernels: none -> 277 us  [on_device(): pl.pallas_call(functools.partial(kernel, (micros, depth, layers, zsize, c...]
    ppermute x23 -> x0, waiting for transfers between devices: 240 us -> none  [shifted(): return lax.ppermute(value, axis, pairs)]
    all_to_all x46 -> x0, starting transfers between devices: 197 us -> none  [the longest x23 99.3 us: run_experts(): lax.all_to_all(outgoing, 'expert', split_axis=0, concat_axis=0, tiled=True)]
    dot_general x16 -> x0, matrix products: 58.3 us -> none  [the longest x8 36.4 us: expert_rows(): jnp.dot(hidden, down_mat, preferred_element_type=jnp.float32)]
    scatter x46 -> x0, other arithmetic: 35.3 us -> none  [the longest x23 18.2 us: advance(): buffer = buffer.at[target[:, 1]].set(normed, mode='drop')]
    ppermute x23 -> x0, starting transfers between devices: 29.7 us -> none  [shifted(): return lax.ppermute(value, axis, pairs)]
    gather x46 -> x0, local copies, waits for them, and re-layouts: 26.6 us -> none  [advance(): own_rows = flat_back[clipped[:, member]]]
  transfers between devices with their start and end apart: 69 -> 0, of which waited for: 69 -> 0; matrix products, arithmetic and copies ran while one was open for 0% -> 0% of each run, Pallas kernels for 0% -> 0%
where the time goes in v1:
time: 289 us; the launch traced here: 287 us
  Pallas kernels  277 us (96%)
  local copies, waits for them, and re-layouts  7.31 us (3%)
    pallas_call x1, Pallas kernels, on_device(): pl.pallas_call(functools.partial(kernel, (micros, depth, layers, zsize, c...  277 us

profile of v1, /device:TPU:30, one launch (start us, length us, event | category | flops | bytes accessed | tf_op | source)
XLA Modules:
  0.0 286.9 jit_solution(16135554009924738204)
XLA Ops:
  0.0 0.7 dynamic-slice_add_fusion
  0.7 0.7 broadcast_select_fusion.1
  1.5 0.1 copy.15
  1.6 0.7 add.30.ctab
  2.3 0.2 copy.16
  2.4 0.7 reshape.23.wtab
  3.2 1.5 copy.22
  4.6 1.0 compare_select_fusion
  5.7 0.1 select_reduce_fusion
  5.8 0.7 reshape.22.dtab
  6.4 1.7 copy.21
  8.1 277.0 %shard_map.91 = bf16[8,8,16,128]{3,2,1,0:T(8,128)(2,1)} custom-call(s32[320]{0:T(512)} %reshape.22.dtab, s32[128]{0:T(128)} %add.30.ctab, f32[256]{0:T(256)} %reshape.23.wtab, bf16[8,8,16,128]{3,2,1,0:T(8,128)(2,1)} %copy.21, f32[8,16,128]{2,1,0:T(8,128)} %bitcast.16, bf16[1,2048,896]{2,1,0:T(8,128)(2,1)} %wg_hbm.1, bf16[1,2048,896]{2,1,0:T(8,128)(2,1)} %wu_hbm.1, ...), custom_call_target="tpu_custom_call" | custom-call | tf_op jit(solution)/shard_map/pallas_call | solution.py:352
  285.1 1.8 reshape.26
  (3 shorter events, 0.0 us)

commit v2 on v1

--- a/solution.py
+++ b/solution.py
@@ -9,7 +9,6 @@
 
 EXPERTS = 4
 LANES = 128
-LAG = 1
 MESH = pl.DeviceIdType.MESH
 BF16 = jnp.bfloat16
 F32 = jnp.float32
@@ -19,7 +18,8 @@
     dims,
     dtab,
     ctab,
-    wtab,
+    wfirst,
+    wsecond,
     tok,
     gain,
     wg_hbm,
@@ -42,6 +42,8 @@
     gu,
     hid,
     summed,
+    states,
+    gains,
     w_sem,
     disp_sem,
     init_sem,
@@ -58,7 +60,7 @@
     st_recv,
 ):
     micros, depth, layers, zsize, cap, sub = dims
-    toks = tok.shape[1]
+    toks = tok.shape[0] // micros
     group = zsize * cap
     ff = wg_hbm.shape[2]
     sec = lax.axis_index("section")
@@ -81,6 +83,9 @@
     for copy in load_weights():
         copy.start()
 
+    def far_first(i):
+        return (z + zsize // 2 - (i + 1) // 2 * (2 * (i % 2) - 1)) % zsize
+
     def taken(ref, sem):
         pltpu.make_async_copy(ref, ref, sem).wait()
 
@@ -93,11 +98,11 @@
 
     def spread(m, table, slot, send_sem, next_layer, may_self):
         for q in range(slots):
-            disp[slot, q] = normed[dtab[table + m * slots + q]]
+            disp[slot, q] = normed[dtab[table, m, q]]
 
         def one(i, carry):
-            to_col = i // zsize
-            to_z = (z + i) % zsize
+            to_col = i % 2
+            to_z = far_first(i // 2)
             expert = 2 * to_col + to_z // (zsize // 2)
             src = disp.at[slot, pl.ds(expert * cap, cap)]
             dst = arows.at[m, core, pl.ds(z * cap, cap)]
@@ -129,8 +134,8 @@
         lax.fori_loop(0, 2 * zsize, one, 0)
 
     def enter(m):
-        normalize(tok[m], gain[0])
-        spread(m, micros * slots, micros + m, init_sem, 0, True)
+        normalize(xbuf[m], gains[0])
+        spread(m, 1, micros + m, init_sem, 0, True)
 
     def x_copy(m):
         return pltpu.make_async_remote_copy(
@@ -145,7 +150,7 @@
     def state_copy(m):
         return pltpu.make_async_remote_copy(
             src_ref=stage.at[m, 1 - core],
-            dst_ref=out.at[m],
+            dst_ref=states.at[m],
             send_sem=st_send.at[m],
             recv_sem=st_recv.at[m],
             device_id=(2 * layer + 1 - core, g),
@@ -173,6 +178,11 @@
         )
 
     def experts(m):
+        def place(part):
+            at = pl.multiple_of(part * group * sub, group * sub)
+            wide = arows[m, part].reshape(group * sub, LANES).astype(F32)
+            tall[pl.ds(at, group * sub), :] = wide
+
         taken(arows.at[m, core], a_sem.at[m])
         relay_copy(m).start()
 
@@ -181,24 +191,26 @@
             for copy in load_weights():
                 copy.wait()
 
+        place(core)
         taken(arows.at[m, 1 - core], relay_recv.at[m])
-        tall[...] = arows[m].reshape(2 * group * sub, LANES).astype(F32)
+        place(1 - core)
         for k in range(sub):
             xmat[:, k * LANES : (k + 1) * LANES] = tall[
                 pl.ds(k, 2 * group, stride=sub), :
             ].astype(BF16)
-        width = 2 * LANES
+        width = ff
         for n in range(2 * ff // width):
             cols = slice(n * width, (n + 1) * width)
             gu[:, cols] = jnp.dot(xmat[...], wgu[:, cols], preferred_element_type=F32)
         gate = gu[:, :ff]
         hid[...] = (gate / (1.0 + jnp.exp(-gate)) * gu[:, ff:]).astype(BF16)
+        width = min(depth, 8 * LANES)
         for n in range(depth // width):
             part = jnp.dot(
                 hid[...], wd[:, n * width : (n + 1) * width], preferred_element_type=F32
             )
-            for k in range(2):
-                tall[pl.ds(2 * n + k, 2 * group, stride=sub), :] = part[
+            for k in range(width // LANES):
+                tall[pl.ds(width // LANES * n + k, 2 * group, stride=sub), :] = part[
                     :, k * LANES : (k + 1) * LANES
                 ]
         away = pl.multiple_of((1 - core) * group * sub, group * sub)
@@ -210,7 +222,7 @@
         rsend[m] = (mine + precv[m].astype(F32)).astype(BF16)
 
         def one(i, carry):
-            to_z = (z + i) % zsize
+            to_z = far_first(i)
             src = rsend.at[m, pl.ds(to_z * cap, cap)]
             dst = rrows.at[m, pl.ds((col * zsize + z) * cap, cap)]
             here = owner & (to_z == z)
@@ -250,28 +262,35 @@
             summed[e * cap : (e + 1) * cap] = total.astype(BF16).astype(F32)
         for t in range(toks):
             wide = xbuf[m, t].astype(F32)
-            at = (m * toks + t) * 2
-            chosen = [summed[ctab[at + k]] for k in range(2)]
-            far = micros * toks * 2
-            half = wide + wtab[at] * chosen[0] + wtab[at + 1] * chosen[1]
-            full = half + wtab[far + at] * chosen[0] + wtab[far + at + 1] * chosen[1]
+            chosen = [summed[ctab[m, k, t]] for k in range(2)]
+            half = wide + wfirst[m, 0, t] * chosen[0] + wfirst[m, 1, t] * chosen[1]
+            full = half + wsecond[m, 0, t] * chosen[0] + wsecond[m, 1, t] * chosen[1]
             stage[m, 0, t] = half.astype(BF16)
             stage[m, 1, t] = full.astype(BF16)
 
         @pl.when(layer < layers - 1)
         def _():
-            normalize(stage[m, 1], gain[jnp.minimum(layer + 1, layers - 1)])
+            normalize(stage[m, 1], gains[1])
             spread(m, 0, m, disp_sem, layer + 1, False)
             x_copy(m).start()
 
         state_copy(m).start()
-        out[m] = stage[m, core]
+        states[m] = stage[m, core]
 
     entering = owner & (layer == 0)
+    later = gain[pl.ds(jnp.minimum(layer + 1, layers - 1), 1), :]
+    for k in range(sub):
+        cols = slice(k * LANES, (k + 1) * LANES)
+        gains[0, k : k + 1, :] = gain[0:1, cols]
+        gains[1, k : k + 1, :] = later[:, cols]
 
     @pl.when(entering)
     def _():
-        xbuf[...] = tok[...]
+        rows = micros * toks
+        for k in range(sub):
+            tall[pl.ds(k, rows, stride=sub), :] = tok[:, k * LANES : (k + 1) * LANES].astype(F32)
+        flat = tall[pl.ds(0, rows * sub), :].astype(BF16)
+        xbuf[...] = flat.reshape(micros, toks, sub, LANES)
         enter(0)
 
     def step(i, carry):
@@ -279,17 +298,15 @@
         def _():
             enter(i + 1)
 
-        @pl.when(i < micros)
-        def _():
-            experts(i)
-
-        @pl.when(owner & (i >= LAG))
-        def _():
-            combine(i - LAG)
+        experts(i)
+
+        @pl.when(owner)
+        def _():
+            combine(i)
 
         return carry
 
-    lax.fori_loop(0, micros + LAG, step, 0)
+    lax.fori_loop(0, micros, step, 0)
 
     def finish(m, carry):
         relay_copy(m).wait_send()
@@ -317,6 +334,10 @@
         return carry
 
     lax.fori_loop(0, micros, finish, 0)
+    rows = micros * toks
+    tall[pl.ds(0, rows * sub), :] = states[...].reshape(rows * sub, LANES).astype(F32)
+    for k in range(sub):
+        out[:, k * LANES : (k + 1) * LANES] = tall[pl.ds(k, rows, stride=sub), :].astype(BF16)
 
 
 def on_device(tokens, norm_gain, w_gate, w_up, w_down, expert_ids, slot_ids, dropped, gate_weights):
@@ -337,12 +358,12 @@
     keys = jnp.stack([at_layer(key_all, jnp.minimum(layer + 1, layers - 1)), key_all[0]])
     token_at = jnp.arange(toks, dtype=jnp.int32)[:, None, None]
     hits = keys[..., None] == jnp.arange(slots, dtype=jnp.int32)
-    dtab = jnp.sum(jnp.where(hits, token_at, 0), axis=(2, 3)).reshape(-1)
+    dtab = jnp.sum(jnp.where(hits, token_at, 0), axis=(2, 3))
     ids = at_layer(expert_ids, layer)
-    ctab = (ids * cap + at_layer(slot_ids, layer)).reshape(-1)
+    ctab = (ids * cap + at_layer(slot_ids, layer)).swapaxes(1, 2)
     weigh = jnp.where(at_layer(dropped, layer) == 0, at_layer(gate_weights, layer), 0.0)
-    first = ids < EXPERTS // 2
-    wtab = jnp.stack([jnp.where(first, weigh, 0.0), jnp.where(first, 0.0, weigh)]).reshape(-1)
+    wfirst = jnp.where(ids < EXPERTS // 2, weigh, 0.0).swapaxes(1, 2)
+    wsecond = jnp.where(ids < EXPERTS // 2, 0.0, weigh).swapaxes(1, 2)
 
     smem = pl.BlockSpec(memory_space=pltpu.SMEM)
     vmem = pl.BlockSpec(memory_space=pltpu.VMEM)
@@ -351,8 +372,8 @@
     dma = pltpu.SemaphoreType.DMA
     states = pl.pallas_call(
         functools.partial(kernel, (micros, depth, layers, zsize, cap, sub)),
-        out_shape=jax.ShapeDtypeStruct((micros, toks) + tile, BF16),
-        in_specs=[smem, smem, smem, vmem, vmem, hbm, hbm, hbm],
+        out_shape=jax.ShapeDtypeStruct((micros * toks, depth), BF16),
+        in_specs=[smem, smem, smem, smem, vmem, vmem, hbm, hbm, hbm],
         out_specs=vmem,
         scratch_shapes=[
             pltpu.VMEM((depth, 2 * ff), BF16),
@@ -366,11 +387,13 @@
             pltpu.VMEM((micros, group) + tile, BF16),
             pltpu.VMEM((micros, group) + tile, BF16),
             pltpu.VMEM((micros, group) + tile, BF16),
-            pltpu.VMEM((2 * group * sub, LANES), F32),
+            pltpu.VMEM((max(2 * group, micros * toks) * sub, LANES), F32),
             pltpu.VMEM((2 * group, depth), BF16),
             pltpu.VMEM((2 * group, 2 * ff), F32),
             pltpu.VMEM((2 * group, ff), BF16),
             pltpu.VMEM((slots,) + tile, F32),
+            pltpu.VMEM((micros, toks) + tile, BF16),
+            pltpu.VMEM((2,) + tile, F32),
             dma((3,)),
         ]
         + [dma((micros,))] * 13,
@@ -380,9 +403,10 @@
     )(
         dtab,
         ctab,
-        wtab,
-        tokens.reshape((micros, toks) + tile),
-        norm_gain.reshape((layers,) + tile),
+        wfirst,
+        wsecond,
+        tokens.reshape(micros * toks, depth),
+        norm_gain,
         w_gate,
         w_up,
         w_down,

time: 289 us -> 272 us (0.941)
  Pallas kernels: 277 us -> 264 us
    pallas_call x1, Pallas kernels: 277 us -> 264 us  [on_device(): pl.pallas_call(functools.partial(kernel, (micros, depth, layers, zsize, c...]
    reshape x3 -> x0, local copies, waits for them, and re-layouts: 3.18 us -> none  [the longest x1 1.77 us: on_device(): return states.reshape(1, micros, toks, depth)]
where the time goes in v2:
time: 272 us
  Pallas kernels  264 us (97%)
  local copies, waits for them, and re-layouts  5.74 us (2%)
    pallas_call x1, Pallas kernels, on_device(): pl.pallas_call(functools.partial(kernel, (micros, depth, layers, zsize, c...  264 us

profile of v2, /device:TPU:30, one launch (start us, length us, event | category | flops | bytes accessed | tf_op | source)
XLA Modules:
  0.0 271.6 jit_solution(3646212071741091161)
XLA Ops:
  0.0 0.0 copy-start
  0.0 0.8 copy-done
  0.8 0.7 constant_dynamic-slice_fusion.3
  1.5 0.7 constant_dynamic-slice_fusion.1
  2.3 0.6 copy.52
  2.9 0.6 copy.50
  3.5 0.6 copy.51
  4.1 1.0 compare_select_fusion
  5.1 0.7 select_reduce_fusion.dtab
  5.8 264.1 %shard_map.91 = bf16[64,2048]{1,0:T(8,128)(2,1)} custom-call(s32[2,8,20]{2,1,0:T(8,128)} %select_reduce_fusion.dtab, s32[8,2,8]{2,1,0:T(2,128)} %bitcast.19, f32[8,2,8]{2,1,0:T(2,128)} %bitcast.21, f32[8,2,8]{2,1,0:T(2,128)} %bitcast.20, bf16[64,2048]{1,0:T(8,128)(2,1)} %bitcast.18, f32[8,2048]{1,0:T(8,128)} %gain.1, bf16[1,2048,896]{2,1,0:T(8,128)(2,1)} %wg_hbm.1, ...), custom_call_target="tpu_custom_call" | custom-call | tf_op jit(solution)/shard_map/pallas_call | solution.py:373
  269.9 1.7 copy.54
  (6 shorter events, 0.0 us)
Async XLA Ops:
  0.0 0.8 copy-start

commit v3 on v2

--- a/solution.py
+++ b/solution.py
@@ -83,6 +83,47 @@
     for copy in load_weights():
         copy.start()
 
+    def greet(section, index):
+        pl.semaphore_signal(
+            pltpu.get_barrier_semaphore(),
+            inc=1,
+            device_id=(section, index),
+            device_id_type=MESH,
+        )
+
+    def greet_plane(section):
+        def one(i, carry):
+            @pl.when((section != sec) | (i != z))
+            def _():
+                greet(section, 2 * i + core)
+
+            return carry
+
+        lax.fori_loop(0, zsize, one, 0)
+
+    greet(sec, partner)
+
+    @pl.when(owner)
+    def _():
+        greet_plane(2 * layer)
+        greet_plane(2 * layer + 1)
+
+    @pl.when(jnp.logical_not(owner) & (layer == 0))
+    def _():
+        greet_plane(core)
+
+    @pl.when(layer > 0)
+    def _():
+        greet_plane(2 * (layer - 1) + core)
+
+    @pl.when(jnp.logical_not(owner) & (layer > 0))
+    def _():
+        greet(2 * layer + core, g)
+
+    own_greets = jnp.where(layer == 0, 2 * zsize, zsize + 1)
+    next_greets = jnp.where(layer < layers - 1, 2 * zsize, 0)
+    greets = jnp.where(owner, own_greets + next_greets, 1 + zsize)
+
     def far_first(i):
         return (z + zsize // 2 - (i + 1) // 2 * (2 * (i % 2) - 1)) % zsize
 
@@ -277,6 +318,7 @@
         state_copy(m).start()
         states[m] = stage[m, core]
 
+    pl.semaphore_wait(pltpu.get_barrier_semaphore(), greets)
     entering = owner & (layer == 0)
     later = gain[pl.ds(jnp.minimum(layer + 1, layers - 1), 1), :]
     for k in range(sub):
@@ -398,7 +440,7 @@
         ]
         + [dma((micros,))] * 13,
         compiler_params=pltpu.CompilerParams(
-            has_side_effects=True, vmem_limit_bytes=60 * 1024 * 1024
+            collective_id=0, has_side_effects=True, vmem_limit_bytes=60 * 1024 * 1024
         ),
     )(
         dtab,

time: 272 us -> 266 us (0.978)
  Pallas kernels: 264 us -> 258 us
    pallas_call x1, Pallas kernels: 264 us -> 258 us  [on_device(): pl.pallas_call(functools.partial(kernel, (micros, depth, layers, zsize, c...]
where the time goes in v3:
time: 266 us; the launch traced here: 265 us
  Pallas kernels  258 us (97%)
  local copies, waits for them, and re-layouts  5.74 us (2%)
    pallas_call x1, Pallas kernels, on_device(): pl.pallas_call(functools.partial(kernel, (micros, depth, layers, zsize, c...  258 us

profile of v3, /device:TPU:30, one launch (start us, length us, event | category | flops | bytes accessed | tf_op | source)
XLA Modules:
  0.0 265.4 jit_solution(4857418100225066183)
XLA Ops:
  0.0 0.0 copy-start
  0.0 0.8 copy-done
  0.8 0.7 constant_dynamic-slice_fusion.3
  1.5 0.7 constant_dynamic-slice_fusion.1
  2.3 0.6 copy.52
  2.9 0.6 copy.50
  3.5 0.6 copy.51
  4.1 1.0 compare_select_fusion
  5.1 0.7 select_reduce_fusion.dtab
  5.8 257.9 %shard_map.91 = bf16[64,2048]{1,0:T(8,128)(2,1)} custom-call(s32[2,8,20]{2,1,0:T(8,128)} %select_reduce_fusion.dtab, s32[8,2,8]{2,1,0:T(2,128)} %bitcast.19, f32[8,2,8]{2,1,0:T(2,128)} %bitcast.21, f32[8,2,8]{2,1,0:T(2,128)} %bitcast.20, bf16[64,2048]{1,0:T(8,128)(2,1)} %bitcast.18, f32[8,2048]{1,0:T(8,128)} %gain.1, bf16[1,2048,896]{2,1,0:T(8,128)(2,1)} %wg_hbm.1, ...), custom_call_target="tpu_custom_call" | custom-call | tf_op jit(solution)/shard_map/pallas_call | solution.py:415
  263.7 1.7 copy.54
  (6 shorter events, 0.0 us)
Async XLA Ops:
  0.0 0.8 copy-start

commit v4 on v3

--- a/solution.py
+++ b/solution.py
@@ -229,7 +229,7 @@
 
         @pl.when(m == 0)
         def _():
-            for copy in load_weights():
+            for copy in load_weights()[:2]:
                 copy.wait()
 
         place(core)
@@ -245,6 +245,11 @@
             gu[:, cols] = jnp.dot(xmat[...], wgu[:, cols], preferred_element_type=F32)
         gate = gu[:, :ff]
         hid[...] = (gate / (1.0 + jnp.exp(-gate)) * gu[:, ff:]).astype(BF16)
+
+        @pl.when(m == 0)
+        def _():
+            load_weights()[2].wait()
+
         width = min(depth, 8 * LANES)
         for n in range(depth // width):
             part = jnp.dot(
@@ -318,7 +323,6 @@
         state_copy(m).start()
         states[m] = stage[m, core]
 
-    pl.semaphore_wait(pltpu.get_barrier_semaphore(), greets)
     entering = owner & (layer == 0)
     later = gain[pl.ds(jnp.minimum(layer + 1, layers - 1), 1), :]
     for k in range(sub):
@@ -333,6 +337,11 @@
             tall[pl.ds(k, rows, stride=sub), :] = tok[:, k * LANES : (k + 1) * LANES].astype(F32)
         flat = tall[pl.ds(0, rows * sub), :].astype(BF16)
         xbuf[...] = flat.reshape(micros, toks, sub, LANES)
+
+    pl.semaphore_wait(pltpu.get_barrier_semaphore(), greets)
+
+    @pl.when(entering)
+    def _():
         enter(0)
 
     def step(i, carry):

time: 266 us -> 266 us (level)
  no operation moved by 1% of the time
where the time goes in v4:
time: 266 us
  Pallas kernels  259 us (97%)
  local copies, waits for them, and re-layouts  5.74 us (2%)
    pallas_call x1, Pallas kernels, on_device(): pl.pallas_call(functools.partial(kernel, (micros, depth, layers, zsize, c...  259 us

profile of v4, /device:TPU:30, one launch (start us, length us, event | category | flops | bytes accessed | tf_op | source)
XLA Modules:
  0.0 266.0 jit_solution(12107981362332327615)
XLA Ops:
  0.0 0.0 copy-start
  0.0 0.8 copy-done
  0.8 0.7 constant_dynamic-slice_fusion.3
  1.5 0.7 constant_dynamic-slice_fusion.1
  2.3 0.6 copy.52
  2.9 0.6 copy.50
  3.5 0.6 copy.51
  4.1 1.0 compare_select_fusion
  5.1 0.7 select_reduce_fusion.dtab
  5.8 258.5 %shard_map.91 = bf16[64,2048]{1,0:T(8,128)(2,1)} custom-call(s32[2,8,20]{2,1,0:T(8,128)} %select_reduce_fusion.dtab, s32[8,2,8]{2,1,0:T(2,128)} %bitcast.19, f32[8,2,8]{2,1,0:T(2,128)} %bitcast.21, f32[8,2,8]{2,1,0:T(2,128)} %bitcast.20, bf16[64,2048]{1,0:T(8,128)(2,1)} %bitcast.18, f32[8,2048]{1,0:T(8,128)} %gain.1, bf16[1,2048,896]{2,1,0:T(8,128)(2,1)} %wg_hbm.1, ...), custom_call_target="tpu_custom_call" | custom-call | tf_op jit(solution)/shard_map/pallas_call | solution.py:424
  264.3 1.7 copy.54
  (6 shorter events, 0.0 us)
Async XLA Ops:
  0.0 0.8 copy-start
